TPU v7x, 8 devices: a whole 2x2x1 slice. The times are simulated.
8 devices in a mesh: slab: 1 (over z), coil: 2 (over y), rows: 4 (over x, core).
Axes of the slice: x: 2, y: 2, z: 1, core: 2. Of those that a mesh axis runs over, the one named last changes fastest.
Arguments:
- kspace: float32 [2, 8, 8192], P(None, 'coil', ('slab', 'rows'))
- weight_row: float32 [6, 8192], P(None, ('slab', 'rows'))
- weight_col: float32 [6, 8192], P(None, ('slab', 'rows'))
- grid_row: int32 [8192], P(('slab', 'rows'))
- grid_col: int32 [8192], P(('slab', 'rows'))
- valid_count: int32 [4], P(('slab', 'rows'))
- coil_maps: float32 [2, 8, 512, 512], P(None, 'coil', 'slab', 'rows')
- deapod: float32 [512], replicated
Outputs:
- output: float32 [2, 512, 512], P(None, ('slab', 'coil'), 'rows')
All inputs are finite; a program needn't handle non-finite values.
Results may differ from a plain program's by a relative error of at most 0.001.
Values are sent between devices in bfloat16 or wider.
A program may use at most 1 GiB of HBM per device.

v0:
```python
import math
import functools
import numpy as np
import jax
import jax.numpy as jnp
from jax import lax
from jax.experimental import pallas as pl
from jax.experimental.pallas import tpu as pltpu
from jax.sharding import PartitionSpec as P

F32 = jnp.float32
BF = jnp.bfloat16
NT = (((1,), (1,)), ((), ()))
KC = 512
GRID = 1024
SAMPLES = 2048
RUN = 256
WIN = 16


def tables(n_img):
    n_grid = 2 * n_img
    pix = np.arange(n_img) - n_img // 2
    freq = np.arange(n_grid) - n_img
    ang = np.mod(pix[:, None] * freq[None, :], n_grid) * (2.0 * math.pi / n_grid)
    return np.stack([np.cos(ang), np.sin(ang)]).astype(np.float32).astype(BF)


def payload(y_ref, wy_ref, wx_ref, key_ref, pay, clear=None):
    @pl.loop(0, SAMPLES // KC)
    def _(s):
        cols = pl.ds(pl.multiple_of(s * KC, KC), KC)
        sub = lax.broadcasted_iota(jnp.int32, (16, KC), 0)
        if clear is not None:
            clear[:, pl.ds(pl.multiple_of(s * 176, 16), 176), :] = jnp.zeros((2, 176, GRID), F32)
        key = key_ref[:, cols]
        r0 = (key >> 10) + 1
        counted = r0 > 0
        t = jnp.where(counted, (sub >> 2) - (r0 & 3), 100)
        for q in range(2):
            y16 = jnp.zeros((16, KC), F32)
            for c in range(4):
                y16 = jnp.where((sub & 3) == c, y_ref[q, c:c + 1, cols], y16)
            coef = [y16 * wy_ref[a:a + 1, cols] for a in range(6)]
            for j in range(3):
                e = jnp.zeros((16, KC), F32)
                for a in range(6):
                    if -3 <= a - 4 * j <= 3:
                        e = jnp.where(t == a - 4 * j, coef[a], e)
                pay[48 * q + 16 * j:48 * q + 16 * j + 16, cols] = e.astype(BF)
        c0 = ((key & (GRID - 1)) + (GRID - 3)) & (GRID - 1)
        wx = wx_ref[:, cols].astype(F32)
        tc = jnp.where(counted, sub - (c0 & 15), 100)
        for j in range(2):
            e = jnp.zeros((16, KC), F32)
            for b in range(6):
                e = jnp.where(tc == b - 16 * j, wx[b:b + 1], e)
            pay[96 + 16 * j:112 + 16 * j, cols] = e.astype(BF)
        pay[128:144, cols] = jnp.broadcast_to(((r0 >> 2) + 1).astype(F32), (16, KC)).astype(BF)
        pay[144:160, cols] = jnp.broadcast_to((c0 >> 4).astype(F32), (16, KC)).astype(BF)


def iota16():
    return lax.broadcasted_iota(jnp.int32, (16, 1), 0).astype(F32)


def tiles(ch):
    first = 4 * (ch // 2) + ch % 2
    return first, first + 2


def ranks(key_ref, oh, rank):
    n_chunk = SAMPLES // RUN
    one, zero = jnp.ones((), BF), jnp.zeros((), BF)
    for ch in range(n_chunk):
        for k, t in enumerate(tiles(ch)):
            bucket = jnp.broadcast_to((((key_ref[:, 128 * t:128 * t + 128] >> 10) + 1) >> 2).astype(F32), (16, 128)).astype(BF)
            for g in range(5):
                oh[80 * ch + 16 * g:80 * ch + 16 * g + 16, 128 * k:128 * k + 128] = jnp.where(bucket == (iota16() + 16 * g).astype(BF), one, zero)
    lower = lax.broadcasted_iota(jnp.int32, (RUN, RUN + 128), 0)
    upper = lax.broadcasted_iota(jnp.int32, (RUN, RUN + 128), 1)
    tri = jnp.where((lower < upper) | (upper >= RUN), 1.0, 0.0).astype(BF)
    pre = jnp.dot(oh[...], tri, preferred_element_type=F32)
    counts = [pre[80 * ch:80 * ch + 80, RUN:] for ch in range(n_chunk)]
    strict = jnp.where(lax.broadcasted_iota(jnp.int32, (80, 80), 1) < lax.broadcasted_iota(jnp.int32, (80, 80), 0), 1.0, 0.0).astype(BF)
    for h in range(2):
        total = counts[h]
        for ch in range(h + 2, n_chunk, 2):
            total = total + counts[ch]
        high = jnp.floor(total * (1.0 / 256.0))
        low = total - 256.0 * high
        base = 256.0 * jnp.dot(strict, high.astype(BF), preferred_element_type=F32) + jnp.dot(strict, low.astype(BF), preferred_element_type=F32)
        for ch in range(h, n_chunk, 2):
            for k, t in enumerate(tiles(ch)):
                place = pre[80 * ch:80 * ch + 80, 128 * k:128 * k + 128] + base
                place = jnp.sum(oh[80 * ch:80 * ch + 80, 128 * k:128 * k + 128].astype(F32) * place, axis=0, keepdims=True)
                place = jnp.where(key_ref[:, 128 * t:128 * t + 128] >= 0, place, -1.0)
                rank[128 * t:128 * t + 128, :] = jnp.broadcast_to(place, (128, 128)).T
            base = base + counts[ch]


def reorder(sp, pay, rank, d_ref):
    lane = lax.broadcasted_iota(jnp.int32, (1, 128), 1).astype(F32)
    one, zero = jnp.ones((), BF), jnp.zeros((), BF)
    for h in range(2):
        total = None
        for ch in range(h, SAMPLES // RUN, 2):
            rows = []
            for t in tiles(ch):
                place = (rank[128 * t:128 * t + 128, :] - (sp * 256).astype(F32)).astype(BF)
                rows.append(jnp.concatenate([jnp.where(place == (lane + 128 * k).astype(BF), one, zero) for k in range(2)], axis=1))
            block = jnp.concatenate(rows, axis=0)
            values = jnp.concatenate([pay[:, 128 * t:128 * t + 128] for t in tiles(ch)], axis=1)
            part = jnp.dot(values, block, preferred_element_type=F32)
            total = part if total is None else total + part
        total = total.astype(BF)
        for k in range(2):
            d_ref[2 * sp + k, :, 128 * h:128 * h + 128] = total[:, 128 * k:128 * k + 128]


def exchange_kernel(y_ref, wy_ref, wx_ref, iy_ref, ix_ref, n_ref, y_out, wy_out, wx_out, key_out, key_own, d_out,
                    y_in, wy_in, wx_in, iy_in, ix_in, wx_bf, pay, oh, rank, loc, ssem, rsem):
    row_id = lax.axis_index('rows')
    other = {'rows': (row_id + 2) % 4}
    barrier = pltpu.get_barrier_semaphore()
    pl.semaphore_signal(barrier, inc=1, device_id=other, device_id_type=pl.DeviceIdType.MESH)
    pairs = [(iy_ref, iy_in), (ix_ref, ix_in), (wx_ref, wx_in), (wy_ref, wy_in), (y_ref, y_in)]
    locs = [pltpu.make_async_copy(a, b, loc.at[i]) for i, (a, b) in enumerate(pairs)]
    for cp in locs:
        cp.start()
    moves = [(y_ref, y_out), (wy_ref, wy_out), (key_own, key_out), (wx_bf, wx_out)]
    sends = [pltpu.make_async_remote_copy(src_ref=a, dst_ref=b, send_sem=ssem.at[i], recv_sem=rsem.at[i], device_id=other, device_id_type=pl.DeviceIdType.MESH) for i, (a, b) in enumerate(moves)]
    pl.semaphore_wait(barrier, 1)
    sends[0].start()
    sends[1].start()
    for cp in locs[:3]:
        cp.wait()
    slot = lax.broadcasted_iota(jnp.int32, iy_in.shape, 1)
    key_own[...] = jnp.where(slot < n_ref[0], (iy_in[...] - row_id * 256) * GRID + ix_in[...], -1000 * GRID)
    wx_bf[...] = wx_in[...].astype(BF)
    sends[2].start()
    sends[3].start()
    for cp in locs[3:]:
        cp.wait()
    payload(y_in, wy_in, wx_bf, key_own, pay)
    ranks(key_own, oh, rank)

    @pl.loop(0, SAMPLES // RUN // 2)
    def _(sp):
        reorder(sp, pay, rank, d_out)

    for cp in sends:
        cp.wait()


def sort_scratch():
    return [pltpu.VMEM((160, SAMPLES), BF), pltpu.VMEM((80 * (SAMPLES // RUN), RUN), BF), pltpu.VMEM((SAMPLES, 128), F32)]


def exchange(y, wy, wx, iy, ix, n):
    vm = pl.BlockSpec(memory_space=pltpu.VMEM)
    anym = pl.BlockSpec(memory_space=pl.ANY)
    dma = pltpu.SemaphoreType.DMA
    shape = jax.ShapeDtypeStruct
    return pl.pallas_call(
        exchange_kernel,
        out_shape=(shape(y.shape, F32), shape(wy.shape, F32), shape(wx.shape, BF), shape(iy.shape, jnp.int32), shape(iy.shape, jnp.int32), shape((SAMPLES // RUN, 160, RUN), BF)),
        in_specs=[anym] * 5 + [pl.BlockSpec(memory_space=pltpu.SMEM)],
        out_specs=(vm,) * 6,
        scratch_shapes=[pltpu.VMEM(v.shape, v.dtype) for v in (y, wy, wx, iy, ix)] + [pltpu.VMEM(wx.shape, BF)] + sort_scratch() + [dma((5,)), dma((4,)), dma((4,))],
        compiler_params=pltpu.CompilerParams(vmem_limit_bytes=12 * 2**20, collective_id=1, has_side_effects=True),
        cost_estimate=pl.CostEstimate(flops=10**9, bytes_accessed=10**6, transcendentals=0),
        name='exchange',
    )(y, wy, wx, iy, ix, n)


def spread_kernel(y_ref, wy_ref, wx_ref, key_ref, key_own, d_own, g_ref, e_ref, d_nb, pay, oh, rank, acc, *b_bufs):
    zero = jnp.zeros((16, RUN), BF)

    def product(d_ref, s, g0, right):
        rel = (d_ref[s, 128:144, :].astype(F32) - (g0 + 1).astype(F32)).astype(BF)
        left = []
        for q in range(2):
            e = [d_ref[s, 48 * q + 16 * j:48 * q + 16 * j + 16, :] for j in range(3)]
            for gi in range(WIN):
                m = [rel == jnp.array(gi - j, BF) for j in range(3)]
                left.append(jnp.where(m[0], e[0], jnp.where(m[1], e[1], jnp.where(m[2], e[2], zero))))
        return lax.dot_general(jnp.concatenate(left, axis=0), right, NT, preferred_element_type=F32)

    def add(g0, prod):
        rows = pl.ds(pl.multiple_of(g0 * 16, 16), 16 * WIN)
        for q in range(2):
            acc[q, rows, :] += prod[16 * WIN * q:16 * WIN * (q + 1)]

    def run_pair(d_ref, sp):
        first, last, prods = [], [], []
        for k in range(2):
            number = d_ref[2 * sp + k, 128:129, :].astype(F32)
            first.append(jnp.min(jnp.where(number > 0.0, number, 66.0)).astype(jnp.int32) - 1)
            last.append(jnp.max(number).astype(jnp.int32) + 1)
        for k in range(2):
            s = 2 * sp + k
            uc = d_ref[s, 144:160, :]
            eb = [d_ref[s, 96 + 16 * j:112 + 16 * j, :] for j in range(2)]
            right = jnp.concatenate([jnp.where(uc == jnp.array(g, BF), eb[0], jnp.where(uc == jnp.array((g - 1) % 64, BF), eb[1], zero)) for g in range(64)], axis=0)
            b_bufs[k][...] = right
            prods.append(product(d_ref, s, first[k], right))
        for k in range(2):
            add(first[k], prods[k])
        for k in range(2):
            @pl.loop(1, (last[k] - first[k] + WIN) // WIN)
            def _(w):
                g0 = first[k] + WIN * w
                add(g0, product(d_ref, 2 * sp + k, g0, b_bufs[k][...]))

    def block(o, d_ref, n_runs):
        if o:
            acc[:, :1056] = jnp.zeros((2, 1056, GRID), F32)


        @pl.loop(0, (n_runs + 1) // 2)
        def _(sp):
            run_pair(d_ref, sp)

        for q in range(2):
            e_ref[o, q, 0:32] = acc[q, 0:32, :]
            e_ref[o, q, 32:64] = acc[q, 1024:1056, :]
            g_ref[o, :, GRID * q:GRID * (q + 1)] = acc[q, 16:1040, :].astype(BF)

    n_own, n_nb = [(jnp.sum(jnp.where(k[...] >= 0, 1.0, 0.0)).astype(jnp.int32) + (RUN - 1)) // RUN for k in (key_own, key_ref)]
    payload(y_ref, wy_ref, wx_ref, key_ref, pay, acc)
    acc[:, 704:1056] = jnp.zeros((2, 352, GRID), F32)
    ranks(key_ref, oh, rank)

    @pl.loop(0, (n_nb + 1) // 2)
    def _(sp):
        reorder(sp, pay, rank, d_nb)

    block(0, d_own, n_own)
    block(1, d_nb, n_nb)


def spread(y, wy, wx, key, key_own, d_own):
    vm = pl.BlockSpec(memory_space=pltpu.VMEM)
    return pl.pallas_call(
        spread_kernel,
        out_shape=(jax.ShapeDtypeStruct((2, 1024, 2 * GRID), BF), jax.ShapeDtypeStruct((2, 2, 64, GRID), F32)),
        in_specs=[vm] * 6,
        out_specs=(vm, vm),
        scratch_shapes=[pltpu.VMEM((SAMPLES // RUN, 160, RUN), BF)] + sort_scratch() + [
            pltpu.VMEM((2, 16 * (66 + WIN), GRID), F32),
            pltpu.VMEM((GRID, RUN), BF),
            pltpu.VMEM((GRID, RUN), BF),
        ],
        compiler_params=pltpu.CompilerParams(vmem_limit_bytes=28 * 2**20),
        cost_estimate=pl.CostEstimate(flops=13 * 10**9, bytes_accessed=4 * 2**20, transcendentals=0),
        name='spread',
    )(y, wy, wx, key, key_own, d_own)


def combine_kernel(gg, ee, tab, maps, dd, out_ref, hbuf, hs, ge, rx, s_all, part, near, far, scale,
                   esend, erecv, ssend, srecv, hsend, hrecv, ysend, yrecv, nsend, nrecv):
    row_id = lax.axis_index('rows')
    y_id = lax.axis_index('coil')
    core = row_id % 2
    x_id = row_id // 2
    sib_row = row_id + 1 - 2 * core
    sib = {'rows': sib_row}
    blocks = [row_id, (row_id + 2) % 4]

    barrier = pltpu.get_barrier_semaphore()
    for dev in (sib, {'coil': 1 - y_id}, {'coil': 1 - y_id, 'rows': sib_row}):
        pl.semaphore_signal(barrier, inc=1, device_id=dev, device_id_type=pl.DeviceIdType.MESH)

    def rows_of(a, c):
        return pl.ds(pl.multiple_of(256 * a + 128 * c, 128), 128)

    for a in range(2):
        s_all[core, a] = maps[:, :, rows_of(a, core), :]
    row_scale = jnp.broadcast_to(dd[:, pl.ds(pl.multiple_of(y_id * 256, 256), 256)], (128, 256)).T
    scale[...] = row_scale * dd[:, pl.ds(pl.multiple_of(row_id * 128, 128), 128)]
    pl.semaphore_wait(barrier, 3)

    def remote(src, dst, send, recv, dev):
        return pltpu.make_async_remote_copy(src_ref=src, dst_ref=dst, send_sem=send, recv_sem=recv, device_id=dev, device_id_type=pl.DeviceIdType.MESH)

    e_copies = []
    for o in range(2):
        low = o * core + (1 - o) * (1 - core)
        high = o * (1 - core) + (1 - o) * core
        for k, (slot, end, row0) in enumerate(((low, 1, 0), (high, 0, 48))):
            e_copies.append(remote(ee.at[o, :, pl.ds(row0, 16)], rx.at[slot, end], esend.at[2 * o + k], erecv.at[slot, end], sib))
    for cp in e_copies:
        cp.start()
    s_copies = [remote(maps.at[:, :, rows_of(a, 1 - core)], s_all.at[core, a], ssend.at[a], srecv.at[a], sib) for a in range(2)]
    for cp in s_copies:
        cp.start()

    def columns(hc, lhs):
        cols = pl.ds(pl.multiple_of(x_id * 256 + hc * 128, 128), 128)
        t2 = jnp.concatenate([tab[0, cols, :], tab[1, cols, :]], axis=0)
        prod = lax.dot_general(lhs, t2, NT, preferred_element_type=F32)
        n = lhs.shape[0] // 2
        return prod[:n, :128] - prod[n:, 128:], prod[:n, 128:] + prod[n:, :128]

    def transform(hc, o, k):
        for j in range(2):
            rows = slice(512 * k + 256 * j, 512 * k + 256 * j + 256)
            pair = columns(hc, jnp.concatenate([gg[o, rows, :GRID], gg[o, rows, GRID:]], axis=0))
            for e in range(2):
                hs[o, e, rows] = pair[e]

    def take_halos():
        for cp in e_copies:
            cp.wait_send()
        for o in range(2):
            for end in range(2):
                remote(rx.at[o, end], rx.at[o, end], esend.at[2 * o + end], erecv.at[o, end], sib).wait_recv()
                for q in range(2):
                    ge[64 * q + 32 * o + 16 * end:64 * q + 32 * o + 16 * end + 16, :] = (ee[o, q, 16 + 16 * end:32 + 16 * end, :] + rx[o, end, q]).astype(BF)

    def patch(hc):
        return columns(hc, ge[...])

    def piece(hc, o, k):
        return remote(hbuf.at[hc, blocks[o], :, pl.ds(128 * k, 128)], hbuf.at[hc, blocks[o], :, pl.ds(128 * k, 128)], hsend.at[hc, o, k], hrecv.at[hc, o, k], sib)

    h_copies = [[piece(hc, o, k) for o in range(2) for k in range(2)] for hc in range(2)]

    def send(hc, o, k, pair):
        for e in range(2):
            hs[o, e, 1008 * k:1008 * k + 16] = pair[e][32 * o + 16 * k:32 * o + 16 * k + 16]
            for c in range(4):
                hbuf[hc, blocks[o], e, 128 * k:128 * k + 128, 128 * c:128 * c + 128] = hs[o, e, pl.ds(512 * k + c, 128, stride=4), :].astype(BF)
        h_copies[hc][2 * o + k].start()

    def image(hc, a):
        rows = rows_of(a, core)
        cos, sin = tab[0, rows, :], tab[1, rows, :]
        quarter = [slice(256 * p, 256 * p + 256) for p in range(4)]
        top = jnp.concatenate([v[:, q] for q in quarter for v in (cos, -sin)], axis=1)
        bottom = jnp.concatenate([v[:, q] for q in quarter for v in (sin, cos)], axis=1)
        both = jnp.dot(jnp.concatenate([top, bottom], axis=0), hbuf[hc].reshape(2048, 512), preferred_element_type=F32)
        re, im = both[:128], both[128:]
        xr = jnp.zeros((128, 128), F32)
        xi = jnp.zeros((128, 128), F32)
        for c in range(4):
            ir = re[:, 128 * c:128 * c + 128]
            ii = im[:, 128 * c:128 * c + 128]
            sr = s_all[hc, a, 0, c]
            si = s_all[hc, a, 1, c]
            xr = xr + (sr * ir + si * ii)
            xi = xi + (sr * ii - si * ir)
        part[hc, a, 0] = xr
        part[hc, a, 1] = xi

    y_copies = [remote(part.at[hc, 1 - y_id], far.at[core], ysend.at[hc], yrecv.at[core], {'coil': 1 - y_id, 'rows': 2 * x_id + hc}) for hc in range(2)]
    n_copy = remote(part.at[1 - core, y_id], near, nsend.at[0], nrecv.at[0], sib)

    for k in range(2):
        transform(0, 0, k)
    take_halos()
    pair = patch(0)
    for k in range(2):
        send(0, 0, k, pair)
    for k in range(2):
        transform(0, 1, k)
        send(0, 1, k, pair)
    pair = patch(1)
    for k in range(2):
        transform(1, 0, k)
        send(1, 0, k, pair)
    for cp in s_copies + h_copies[0]:
        cp.wait()
    image(0, 1 - y_id)
    y_copies[0].start()
    for k in range(2):
        transform(1, 1, k)
        send(1, 1, k, pair)
    image(0, y_id)
    for cp in h_copies[1]:
        cp.wait()
    image(1, 1 - y_id)
    y_copies[1].start()
    image(1, y_id)
    n_copy.start()
    for cp in y_copies:
        cp.wait_send()
    n_copy.wait()
    mine = pl.ds(pl.multiple_of(128 * core, 128), 128)
    other = pl.ds(pl.multiple_of(128 * (1 - core), 128), 128)
    for e in range(2):
        out_ref[e, mine] = part[core, y_id, e]
        out_ref[e, other] = near[e]
    for k in range(2):
        remote(far.at[k], far.at[k], ysend.at[k], yrecv.at[k], {'coil': 1 - y_id}).wait_recv()
        sl = slice(128 * k, 128 * k + 128)
        for e in range(2):
            out_ref[e, sl] = (out_ref[e, sl] + far[k, e]) * scale[sl]


def combine(gg, ee, tab, maps, dd):
    vm = pl.BlockSpec(memory_space=pltpu.VMEM)
    dma = pltpu.SemaphoreType.DMA
    return pl.pallas_call(
        combine_kernel,
        out_shape=jax.ShapeDtypeStruct((2, 256, 128), F32),
        in_specs=[vm] * 5,
        out_specs=vm,
        scratch_shapes=[
            pltpu.VMEM((2, 4, 2, 256, 512), BF),
            pltpu.VMEM((2, 2, 1024, 128), F32),
            pltpu.VMEM((128, GRID), BF),
            pltpu.VMEM((2, 2, 2, 16, GRID), F32),
            pltpu.VMEM((2, 2, 2, 4, 128, 128), F32),
            pltpu.VMEM((2, 2, 2, 128, 128), F32),
            pltpu.VMEM((2, 128, 128), F32),
            pltpu.VMEM((2, 2, 128, 128), F32),
            pltpu.VMEM((256, 128), F32),
            dma((4,)), dma((2, 2)), dma((2,)), dma((2,)), dma((2, 2, 2)), dma((2, 2, 2)), dma((2,)), dma((2,)), dma((1,)), dma((1,)),
        ],
        compiler_params=pltpu.CompilerParams(vmem_limit_bytes=24 * 2**20, collective_id=0, has_side_effects=True),
        cost_estimate=pl.CostEstimate(flops=7 * 10**9, bytes_accessed=12 * 2**20, transcendentals=0),
        name='combine',
    )(gg, ee, tab, maps, dd)


def solution(mesh):
    def local_part(kspace, weight_row, weight_col, grid_row, grid_col, valid_count, coil_maps, deapod):
        n_img = deapod.shape[0]
        hbm = [pltpu.with_memory_space_constraint(v, pltpu.HBM) for v in (kspace, weight_row, weight_col, grid_row[None], grid_col[None])]
        stacked = exchange(*hbm, valid_count)
        tab = jnp.asarray(tables(n_img))
        gg, ee = spread(*stacked)
        return combine(gg, ee, tab, coil_maps, deapod[None])

    spec_samples = P(None, 'coil', ('slab', 'rows'))
    spec_weights = P(None, ('slab', 'rows'))
    spec_index = P(('slab', 'rows'))
    return jax.shard_map(local_part, mesh=mesh, in_specs=(spec_samples, spec_weights, spec_weights, spec_index, spec_index, spec_index, P(None, 'coil', 'slab', 'rows'), P()), out_specs=P(None, ('slab', 'coil'), 'rows'), check_vma=False)
```

profile of v0, /device:TPU:0, one launch (start us, length us, event | category | flops | bytes accessed | tf_op | source)
XLA Modules:
  0.0 35.7 jit_solution(13014533841759558630)
XLA Ops:
  0.7 7.9 %exchange.1 = (f32[2,4,2048]{2,1,0:T(4,128)S(1)}, f32[6,2048]{1,0:T(8,128)S(1)}, bf16[6,2048]{1,0:T(8,128)(2,1)S(1)}, s32[1,2048]{1,0:T(1,128)S(1)}, s32[1,2048]...) custom-call(f32[2,4,2048]{2,1,0:T(4,128)} %y_ref.1, f32[6,2048]{1,0:T(8,128)} %wy_ref.1, f32[6,2048]{1,0:T(8,128)} %wx_ref.1, ...), custom_call_target="tpu_custom_call" | custom-call | flops 1000000000 | bytes 1000000 | tf_op jit(solution)/shard_map/exchange/pallas_call | solution.py:165
  8.5 0.0 copy-start
  8.5 0.0 copy-start.1
  8.5 0.0 copy-start.2
  8.5 10.9 %spread.1 = (bf16[2,1024,2048]{2,1,0:T(8,128)(2,1)S(1)}, f32[2,2,64,1024]{3,2,1,0:T(8,128)S(1)}) custom-call(f32[2,4,2048]{2,1,0:T(4,128)S(1)} %get-tuple-element.13.y_ref, f32[6,2048]{1,0:T(8,128)S(1)} %get-tuple-element.14.wy_ref, bf16[6,2048]{1,0:T(8,128)(2,1)S(1)} %get-tuple-element.15.wx_ref, s32[1,2048]{1,0:T(1,128)S(1)} %get-tuple-element.16.key_ref, ...), custom_call_target="tpu_custom_call" | custom-call | flops 12999999488 | bytes 4194304 | tf_op jit(solution)/shard_map/spread/pallas_call | solution.py:245
  19.5 0.0 copy-done
  19.5 0.0 copy-done.1
  19.5 0.0 copy-done.2
  19.5 15.5 %combine.1 = f32[2,256,128]{2,1,0:T(8,128)S(1)} custom-call(bf16[2,1024,2048]{2,1,0:T(8,128)(2,1)S(1)} %get-tuple-element.19.gg, f32[2,2,64,1024]{3,2,1,0:T(8,128)S(1)} %get-tuple-element.20.ee, bf16[2,512,1024]{2,1,0:T(8,128)(2,1)S(1)} %copy-done.2, f32[2,4,512,128]{3,2,1,0:T(8,128)S(1)} %copy-done, f32[1,512]{1,0:T(1,128)S(1)} %bitcast.3), custom_call_target="tpu_custom_call" | custom-call | flops 7000000000 | bytes 12582912 | tf_op jit(solution)/shard_map/combine/pallas_call | solution.py:405
  35.0 0.7 %copy.12 = f32[2,256,128]{2,1,0:T(8,128)} copy(f32[2,256,128]{2,1,0:T(8,128)S(1)} %combine.1) | data formatting | bytes 524288
Async XLA Ops:
  8.5 11.0 %copy-start = (f32[2,4,512,128]{3,2,1,0:T(8,128)S(1)}, f32[2,4,512,128]{3,2,1,0:T(8,128)}, u32[]{:S(2)}) copy-start(f32[2,4,512,128]{3,2,1,0:T(8,128)} %maps.1) | copy-start | bytes 6291460
  8.5 11.0 %copy-start.1 = (f32[512]{0:T(512)S(1)}, f32[512]{0:T(512)}, u32[]{:S(2)}) copy-start(f32[512]{0:T(512)} %param.16) | copy-start | bytes 6148
  8.5 11.0 %copy-start.2 = (bf16[2,512,1024]{2,1,0:T(8,128)(2,1)S(1)}, bf16[2,512,1024]{2,1,0:T(8,128)(2,1)}, u32[]{:S(2)}) copy-start(bf16[2,512,1024]{2,1,0:T(8,128)(2,1)} %constant.2.clone.tab) | copy-start | bytes 6291460
where the time goes:
time: 36.2 us; the launch traced here: 35.7 us
  Pallas kernels  34.2 us (94%)
  local copies, waits for them, and re-layouts  0.72 us (2%)
  between operations  0.72 us (2%)
    pallas_call x1, Pallas kernels, combine(): pl.pallas_call(combine_kernel, out_shape=jax.ShapeDtypeStruct((2, 256, 12...  15.5 us
    pallas_call x1, Pallas kernels, spread(): pl.pallas_call(spread_kernel, out_shape=(jax.ShapeDtypeStruct((2, 1024, 2...  10.9 us
    pallas_call x1, Pallas kernels, exchange(): pl.pallas_call(exchange_kernel, out_shape=(shape(y.shape, F32), shape(wy....  7.85 us
    unnamed x7, local copies, waits for them, and re-layouts  0.72 us

commit v1 on v0

--- a/solution.py
+++ b/solution.py
@@ -264,22 +264,22 @@
     y_id = lax.axis_index('coil')
     core = row_id % 2
     x_id = row_id // 2
-    sib_row = row_id + 1 - 2 * core
-    sib = {'rows': sib_row}
+    sib = {'rows': row_id + 1 - 2 * core}
     blocks = [row_id, (row_id + 2) % 4]
 
     barrier = pltpu.get_barrier_semaphore()
-    for dev in (sib, {'coil': 1 - y_id}, {'coil': 1 - y_id, 'rows': sib_row}):
+    mate = {'coil': 1 - y_id}
+    for dev in (sib, mate):
         pl.semaphore_signal(barrier, inc=1, device_id=dev, device_id_type=pl.DeviceIdType.MESH)
 
     def rows_of(a, c):
         return pl.ds(pl.multiple_of(256 * a + 128 * c, 128), 128)
 
-    for a in range(2):
-        s_all[core, a] = maps[:, :, rows_of(a, core), :]
+    for k in range(2):
+        s_all[core, k] = maps[:, :, rows_of(1 - y_id, k), :]
     row_scale = jnp.broadcast_to(dd[:, pl.ds(pl.multiple_of(y_id * 256, 256), 256)], (128, 256)).T
     scale[...] = row_scale * dd[:, pl.ds(pl.multiple_of(row_id * 128, 128), 128)]
-    pl.semaphore_wait(barrier, 3)
+    pl.semaphore_wait(barrier, 2)
 
     def remote(src, dst, send, recv, dev):
         return pltpu.make_async_remote_copy(src_ref=src, dst_ref=dst, send_sem=send, recv_sem=recv, device_id=dev, device_id_type=pl.DeviceIdType.MESH)
@@ -292,7 +292,7 @@
             e_copies.append(remote(ee.at[o, :, pl.ds(row0, 16)], rx.at[slot, end], esend.at[2 * o + k], erecv.at[slot, end], sib))
     for cp in e_copies:
         cp.start()
-    s_copies = [remote(maps.at[:, :, rows_of(a, 1 - core)], s_all.at[core, a], ssend.at[a], srecv.at[a], sib) for a in range(2)]
+    s_copies = [remote(maps.at[:, :, rows_of(y_id, k)], s_all.at[core, k], ssend.at[k], srecv.at[k], sib) for k in range(2)]
     for cp in s_copies:
         cp.start()
 
@@ -334,8 +334,8 @@
                 hbuf[hc, blocks[o], e, 128 * k:128 * k + 128, 128 * c:128 * c + 128] = hs[o, e, pl.ds(512 * k + c, 128, stride=4), :].astype(BF)
         h_copies[hc][2 * o + k].start()
 
-    def image(hc, a):
-        rows = rows_of(a, core)
+    def image(hc, k):
+        rows = rows_of(y_id + (1 - 2 * y_id) * (1 - core - hc + 2 * core * hc), k)
         cos, sin = tab[0, rows, :], tab[1, rows, :]
         quarter = [slice(256 * p, 256 * p + 256) for p in range(4)]
         top = jnp.concatenate([v[:, q] for q in quarter for v in (cos, -sin)], axis=1)
@@ -347,15 +347,23 @@
         for c in range(4):
             ir = re[:, 128 * c:128 * c + 128]
             ii = im[:, 128 * c:128 * c + 128]
-            sr = s_all[hc, a, 0, c]
-            si = s_all[hc, a, 1, c]
+            sr = s_all[hc, k, 0, c]
+            si = s_all[hc, k, 1, c]
             xr = xr + (sr * ir + si * ii)
             xi = xi + (sr * ii - si * ir)
-        part[hc, a, 0] = xr
-        part[hc, a, 1] = xi
-
-    y_copies = [remote(part.at[hc, 1 - y_id], far.at[core], ysend.at[hc], yrecv.at[core], {'coil': 1 - y_id, 'rows': 2 * x_id + hc}) for hc in range(2)]
-    n_copy = remote(part.at[1 - core, y_id], near, nsend.at[0], nrecv.at[0], sib)
+        part[hc, k, 0] = xr
+        part[hc, k, 1] = xi
+
+        @pl.when(core == hc)
+        def _():
+            y_copies[k].start()
+
+        @pl.when(core != hc)
+        def _():
+            n_copies[k].start()
+
+    y_copies = [remote(part.at[core, k], far.at[k], ysend.at[k], yrecv.at[k], mate) for k in range(2)]
+    n_copies = [remote(part.at[1 - core, k], near.at[k], nsend.at[k], nrecv.at[k], sib) for k in range(2)]
 
     for k in range(2):
         transform(0, 0, k)
@@ -372,31 +380,21 @@
         send(1, 0, k, pair)
     for cp in s_copies + h_copies[0]:
         cp.wait()
-    image(0, 1 - y_id)
-    y_copies[0].start()
+    image(0, 0)
     for k in range(2):
         transform(1, 1, k)
         send(1, 1, k, pair)
-    image(0, y_id)
+    image(0, 1)
     for cp in h_copies[1]:
         cp.wait()
-    image(1, 1 - y_id)
-    y_copies[1].start()
-    image(1, y_id)
-    n_copy.start()
-    for cp in y_copies:
-        cp.wait_send()
-    n_copy.wait()
-    mine = pl.ds(pl.multiple_of(128 * core, 128), 128)
-    other = pl.ds(pl.multiple_of(128 * (1 - core), 128), 128)
-    for e in range(2):
-        out_ref[e, mine] = part[core, y_id, e]
-        out_ref[e, other] = near[e]
-    for k in range(2):
-        remote(far.at[k], far.at[k], ysend.at[k], yrecv.at[k], {'coil': 1 - y_id}).wait_recv()
+    for k in range(2):
+        image(1, k)
+    for k in range(2):
+        n_copies[k].wait()
+        y_copies[k].wait()
         sl = slice(128 * k, 128 * k + 128)
         for e in range(2):
-            out_ref[e, sl] = (out_ref[e, sl] + far[k, e]) * scale[sl]
+            out_ref[e, sl] = (near[k, e] + far[k, e]) * scale[sl]
 
 
 def combine(gg, ee, tab, maps, dd):
@@ -414,10 +412,10 @@
             pltpu.VMEM((2, 2, 2, 16, GRID), F32),
             pltpu.VMEM((2, 2, 2, 4, 128, 128), F32),
             pltpu.VMEM((2, 2, 2, 128, 128), F32),
-            pltpu.VMEM((2, 128, 128), F32),
+            pltpu.VMEM((2, 2, 128, 128), F32),
             pltpu.VMEM((2, 2, 128, 128), F32),
             pltpu.VMEM((256, 128), F32),
-            dma((4,)), dma((2, 2)), dma((2,)), dma((2,)), dma((2, 2, 2)), dma((2, 2, 2)), dma((2,)), dma((2,)), dma((1,)), dma((1,)),
+            dma((4,)), dma((2, 2)), dma((2,)), dma((2,)), dma((2, 2, 2)), dma((2, 2, 2)), dma((2,)), dma((2,)), dma((2,)), dma((2,)),
         ],
         compiler_params=pltpu.CompilerParams(vmem_limit_bytes=24 * 2**20, collective_id=0, has_side_effects=True),
         cost_estimate=pl.CostEstimate(flops=7 * 10**9, bytes_accessed=12 * 2**20, transcendentals=0),

time: 36.2 us -> 36.8 us (1.017)
  the two profiles are of different devices: /device:TPU:0 before, /device:TPU:1 now
where the time goes in v1:
time: 36.8 us; the launch traced here: 37.3 us
  Pallas kernels  35.9 us (98%)
  local copies, waits for them, and re-layouts  0.72 us (2%)
  between operations  0.72 us (2%)
    pallas_call x1, Pallas kernels, combine(): pl.pallas_call(combine_kernel, out_shape=jax.ShapeDtypeStruct((2, 256, 12...  17.2 us
    pallas_call x1, Pallas kernels, spread(): pl.pallas_call(spread_kernel, out_shape=(jax.ShapeDtypeStruct((2, 1024, 2...  12.5 us
    pallas_call x1, Pallas kernels, exchange(): pl.pallas_call(exchange_kernel, out_shape=(shape(y.shape, F32), shape(wy....  6.25 us

profile of v1, /device:TPU:1, one launch (start us, length us, event | category | flops | bytes accessed | tf_op | source)
XLA Modules:
  0.0 37.3 jit_solution(1441448955056754852)
XLA Ops:
  0.7 6.3 %exchange.1 = (f32[2,4,2048]{2,1,0:T(4,128)S(1)}, f32[6,2048]{1,0:T(8,128)S(1)}, bf16[6,2048]{1,0:T(8,128)(2,1)S(1)}, s32[1,2048]{1,0:T(1,128)S(1)}, s32[1,2048]...) custom-call(f32[2,4,2048]{2,1,0:T(4,128)} %y_ref.1, f32[6,2048]{1,0:T(8,128)} %wy_ref.1, f32[6,2048]{1,0:T(8,128)} %wx_ref.1, ...), custom_call_target="tpu_custom_call" | custom-call | flops 1000000000 | bytes 1000000 | tf_op jit(solution)/shard_map/exchange/pallas_call | solution.py:165
  6.9 0.0 copy-start
  6.9 0.0 copy-start.1
  6.9 0.0 copy-start.2
  7.0 12.5 %spread.1 = (bf16[2,1024,2048]{2,1,0:T(8,128)(2,1)S(1)}, f32[2,2,64,1024]{3,2,1,0:T(8,128)S(1)}) custom-call(f32[2,4,2048]{2,1,0:T(4,128)S(1)} %get-tuple-element.13.y_ref, f32[6,2048]{1,0:T(8,128)S(1)} %get-tuple-element.14.wy_ref, bf16[6,2048]{1,0:T(8,128)(2,1)S(1)} %get-tuple-element.15.wx_ref, s32[1,2048]{1,0:T(1,128)S(1)} %get-tuple-element.16.key_ref, ...), custom_call_target="tpu_custom_call" | custom-call | flops 12999999488 | bytes 4194304 | tf_op jit(solution)/shard_map/spread/pallas_call | solution.py:245
  19.4 0.0 copy-done
  19.5 0.0 copy-done.1
  19.5 0.0 copy-done.2
  19.5 17.2 %combine.1 = f32[2,256,128]{2,1,0:T(8,128)S(1)} custom-call(bf16[2,1024,2048]{2,1,0:T(8,128)(2,1)S(1)} %get-tuple-element.19.gg, f32[2,2,64,1024]{3,2,1,0:T(8,128)S(1)} %get-tuple-element.20.ee, bf16[2,512,1024]{2,1,0:T(8,128)(2,1)S(1)} %copy-done.2, f32[2,4,512,128]{3,2,1,0:T(8,128)S(1)} %copy-done, f32[1,512]{1,0:T(1,128)S(1)} %bitcast.3), custom_call_target="tpu_custom_call" | custom-call | flops 7000000000 | bytes 12582912 | tf_op jit(solution)/shard_map/combine/pallas_call | solution.py:403
  36.6 0.7 %copy.12 = f32[2,256,128]{2,1,0:T(8,128)} copy(f32[2,256,128]{2,1,0:T(8,128)S(1)} %combine.1) | data formatting | bytes 524288
Async XLA Ops:
  6.9 12.5 %copy-start = (f32[2,4,512,128]{3,2,1,0:T(8,128)S(1)}, f32[2,4,512,128]{3,2,1,0:T(8,128)}, u32[]{:S(2)}) copy-start(f32[2,4,512,128]{3,2,1,0:T(8,128)} %maps.1) | copy-start | bytes 6291460
  6.9 12.5 %copy-start.1 = (f32[512]{0:T(512)S(1)}, f32[512]{0:T(512)}, u32[]{:S(2)}) copy-start(f32[512]{0:T(512)} %param.16) | copy-start | bytes 6148
  6.9 12.5 %copy-start.2 = (bf16[2,512,1024]{2,1,0:T(8,128)(2,1)S(1)}, bf16[2,512,1024]{2,1,0:T(8,128)(2,1)}, u32[]{:S(2)}) copy-start(bf16[2,512,1024]{2,1,0:T(8,128)(2,1)} %constant.2.clone.tab) | copy-start | bytes 6291460

commit v2 on v0

--- a/solution.py
+++ b/solution.py
@@ -27,12 +27,11 @@
 
 
 def payload(y_ref, wy_ref, wx_ref, key_ref, pay, clear=None):
-    @pl.loop(0, SAMPLES // KC)
-    def _(s):
-        cols = pl.ds(pl.multiple_of(s * KC, KC), KC)
+    for s in range(SAMPLES // KC):
+        cols = slice(s * KC, s * KC + KC)
         sub = lax.broadcasted_iota(jnp.int32, (16, KC), 0)
         if clear is not None:
-            clear[:, pl.ds(pl.multiple_of(s * 176, 16), 176), :] = jnp.zeros((2, 176, GRID), F32)
+            clear[:, 176 * s:176 * s + 176, :] = jnp.zeros((2, 176, GRID), F32)
         key = key_ref[:, cols]
         r0 = (key >> 10) + 1
         counted = r0 > 0
@@ -185,7 +184,7 @@
             for gi in range(WIN):
                 m = [rel == jnp.array(gi - j, BF) for j in range(3)]
                 left.append(jnp.where(m[0], e[0], jnp.where(m[1], e[1], jnp.where(m[2], e[2], zero))))
-        return lax.dot_general(jnp.concatenate(left, axis=0), right, NT, preferred_element_type=F32)
+        return jnp.dot(jnp.concatenate(left, axis=0), right, preferred_element_type=F32)
 
     def add(g0, prod):
         rows = pl.ds(pl.multiple_of(g0 * 16, 16), 16 * WIN)
@@ -203,8 +202,9 @@
             uc = d_ref[s, 144:160, :]
             eb = [d_ref[s, 96 + 16 * j:112 + 16 * j, :] for j in range(2)]
             right = jnp.concatenate([jnp.where(uc == jnp.array(g, BF), eb[0], jnp.where(uc == jnp.array((g - 1) % 64, BF), eb[1], zero)) for g in range(64)], axis=0)
-            b_bufs[k][...] = right
-            prods.append(product(d_ref, s, first[k], right))
+            b_bufs[k][...] = right.T
+        for k in range(2):
+            prods.append(product(d_ref, 2 * sp + k, first[k], b_bufs[k][...]))
         for k in range(2):
             add(first[k], prods[k])
         for k in range(2):
@@ -249,8 +249,8 @@
         out_specs=(vm, vm),
         scratch_shapes=[pltpu.VMEM((SAMPLES // RUN, 160, RUN), BF)] + sort_scratch() + [
             pltpu.VMEM((2, 16 * (66 + WIN), GRID), F32),
-            pltpu.VMEM((GRID, RUN), BF),
-            pltpu.VMEM((GRID, RUN), BF),
+            pltpu.VMEM((RUN, GRID), BF),
+            pltpu.VMEM((RUN, GRID), BF),
         ],
         compiler_params=pltpu.CompilerParams(vmem_limit_bytes=28 * 2**20),
         cost_estimate=pl.CostEstimate(flops=13 * 10**9, bytes_accessed=4 * 2**20, transcendentals=0),

time: 36.2 us -> 36.4 us (level); the launches traced: 35.7 us -> 36.3 us
  Pallas kernels: 34.2 us -> 34.9 us
    pallas_call x1, Pallas kernels: 10.9 us -> 11.5 us  [spread(): pl.pallas_call(spread_kernel, out_shape=(jax.ShapeDtypeStruct((2, 1024, 2...]
where the time goes in v2:
time: 36.4 us; the launch traced here: 36.3 us
  Pallas kernels  34.9 us (96%)
  local copies, waits for them, and re-layouts  0.72 us (2%)
  between operations  0.72 us (2%)
    pallas_call x1, Pallas kernels, combine(): pl.pallas_call(combine_kernel, out_shape=jax.ShapeDtypeStruct((2, 256, 12...  15.5 us
    pallas_call x1, Pallas kernels, spread(): pl.pallas_call(spread_kernel, out_shape=(jax.ShapeDtypeStruct((2, 1024, 2...  11.5 us
    pallas_call x1, Pallas kernels, exchange(): pl.pallas_call(exchange_kernel, out_shape=(shape(y.shape, F32), shape(wy....  7.85 us

profile of v2, /device:TPU:0, one launch (start us, length us, event | category | flops | bytes accessed | tf_op | source)
XLA Modules:
  0.0 36.3 jit_solution(17046103390727832134)
XLA Ops:
  0.7 7.9 %exchange.1 = (f32[2,4,2048]{2,1,0:T(4,128)S(1)}, f32[6,2048]{1,0:T(8,128)S(1)}, bf16[6,2048]{1,0:T(8,128)(2,1)S(1)}, s32[1,2048]{1,0:T(1,128)S(1)}, s32[1,2048]...) custom-call(f32[2,4,2048]{2,1,0:T(4,128)} %y_ref.1, f32[6,2048]{1,0:T(8,128)} %wy_ref.1, f32[6,2048]{1,0:T(8,128)} %wx_ref.1, ...), custom_call_target="tpu_custom_call" | custom-call | flops 1000000000 | bytes 1000000 | tf_op jit(solution)/shard_map/exchange/pallas_call | solution.py:164
  8.5 0.0 copy-start
  8.5 0.0 copy-start.1
  8.5 0.0 copy-start.2
  8.5 11.5 %spread.1 = (bf16[2,1024,2048]{2,1,0:T(8,128)(2,1)S(1)}, f32[2,2,64,1024]{3,2,1,0:T(8,128)S(1)}) custom-call(f32[2,4,2048]{2,1,0:T(4,128)S(1)} %get-tuple-element.13.y_ref, f32[6,2048]{1,0:T(8,128)S(1)} %get-tuple-element.14.wy_ref, bf16[6,2048]{1,0:T(8,128)(2,1)S(1)} %get-tuple-element.15.wx_ref, s32[1,2048]{1,0:T(1,128)S(1)} %get-tuple-element.16.key_ref, ...), custom_call_target="tpu_custom_call" | custom-call | flops 12999999488 | bytes 4194304 | tf_op jit(solution)/shard_map/spread/pallas_call | solution.py:245
  20.1 0.0 copy-done
  20.1 0.0 copy-done.1
  20.1 0.0 copy-done.2
  20.1 15.5 %combine.1 = f32[2,256,128]{2,1,0:T(8,128)S(1)} custom-call(bf16[2,1024,2048]{2,1,0:T(8,128)(2,1)S(1)} %get-tuple-element.19.gg, f32[2,2,64,1024]{3,2,1,0:T(8,128)S(1)} %get-tuple-element.20.ee, bf16[2,512,1024]{2,1,0:T(8,128)(2,1)S(1)} %copy-done.2, f32[2,4,512,128]{3,2,1,0:T(8,128)S(1)} %copy-done, f32[1,512]{1,0:T(1,128)S(1)} %bitcast.3), custom_call_target="tpu_custom_call" | custom-call | flops 7000000000 | bytes 12582912 | tf_op jit(solution)/shard_map/combine/pallas_call | solution.py:405
  35.6 0.7 %copy.12 = f32[2,256,128]{2,1,0:T(8,128)} copy(f32[2,256,128]{2,1,0:T(8,128)S(1)} %combine.1) | data formatting | bytes 524288
Async XLA Ops:
  8.5 11.6 %copy-start = (f32[2,4,512,128]{3,2,1,0:T(8,128)S(1)}, f32[2,4,512,128]{3,2,1,0:T(8,128)}, u32[]{:S(2)}) copy-start(f32[2,4,512,128]{3,2,1,0:T(8,128)} %maps.1) | copy-start | bytes 6291460
  8.5 11.6 %copy-start.1 = (f32[512]{0:T(512)S(1)}, f32[512]{0:T(512)}, u32[]{:S(2)}) copy-start(f32[512]{0:T(512)} %param.16) | copy-start | bytes 6148
  8.5 11.6 %copy-start.2 = (bf16[2,512,1024]{2,1,0:T(8,128)(2,1)S(1)}, bf16[2,512,1024]{2,1,0:T(8,128)(2,1)}, u32[]{:S(2)}) copy-start(bf16[2,512,1024]{2,1,0:T(8,128)(2,1)} %constant.2.clone.tab) | copy-start | bytes 6291460

commit v3 on v2

--- a/solution.py
+++ b/solution.py
@@ -258,7 +258,7 @@
     )(y, wy, wx, key, key_own, d_own)
 
 
-def combine_kernel(gg, ee, tab, maps, dd, out_ref, hbuf, hs, ge, rx, s_all, part, near, far, scale,
+def combine_kernel(gg, ee, tab, maps, dd, out_ref, hbuf, hs, ge, rx, s_all, part, near, far, scale, table,
                    esend, erecv, ssend, srecv, hsend, hrecv, ysend, yrecv, nsend, nrecv):
     row_id = lax.axis_index('rows')
     y_id = lax.axis_index('coil')
@@ -295,11 +295,13 @@
     s_copies = [remote(maps.at[:, :, rows_of(a, 1 - core)], s_all.at[core, a], ssend.at[a], srecv.at[a], sib) for a in range(2)]
     for cp in s_copies:
         cp.start()
+    for hc in range(2):
+        cols = pl.ds(pl.multiple_of(x_id * 256 + hc * 128, 128), 128)
+        table[hc] = jnp.concatenate([tab[0, cols, :], tab[1, cols, :]], axis=0).T
 
     def columns(hc, lhs):
-        cols = pl.ds(pl.multiple_of(x_id * 256 + hc * 128, 128), 128)
-        t2 = jnp.concatenate([tab[0, cols, :], tab[1, cols, :]], axis=0)
-        prod = lax.dot_general(lhs, t2, NT, preferred_element_type=F32)
+        t2 = table[hc]
+        prod = jnp.dot(lhs, t2, preferred_element_type=F32)
         n = lhs.shape[0] // 2
         return prod[:n, :128] - prod[n:, 128:], prod[:n, 128:] + prod[n:, :128]
 
@@ -417,6 +419,7 @@
             pltpu.VMEM((2, 128, 128), F32),
             pltpu.VMEM((2, 2, 128, 128), F32),
             pltpu.VMEM((256, 128), F32),
+            pltpu.VMEM((2, GRID, 256), BF),
             dma((4,)), dma((2, 2)), dma((2,)), dma((2,)), dma((2, 2, 2)), dma((2, 2, 2)), dma((2,)), dma((2,)), dma((1,)), dma((1,)),
         ],
         compiler_params=pltpu.CompilerParams(vmem_limit_bytes=24 * 2**20, collective_id=0, has_side_effects=True),

time: 36.4 us -> 35.6 us (0.978)
  Pallas kernels: 34.9 us -> 34.1 us
    pallas_call x1, Pallas kernels: 15.5 us -> 14.7 us  [combine(): pl.pallas_call(combine_kernel, out_shape=jax.ShapeDtypeStruct((2, 256, 12...]
where the time goes in v3:
time: 35.6 us; the launch traced here: 35.5 us
  Pallas kernels  34.1 us (96%)
  local copies, waits for them, and re-layouts  0.72 us (2%)
  between operations  0.72 us (2%)
    pallas_call x1, Pallas kernels, combine(): pl.pallas_call(combine_kernel, out_shape=jax.ShapeDtypeStruct((2, 256, 12...  14.7 us
    pallas_call x1, Pallas kernels, spread(): pl.pallas_call(spread_kernel, out_shape=(jax.ShapeDtypeStruct((2, 1024, 2...  11.5 us
    pallas_call x1, Pallas kernels, exchange(): pl.pallas_call(exchange_kernel, out_shape=(shape(y.shape, F32), shape(wy....  7.85 us
    unnamed x7, local copies, waits for them, and re-layouts  0.72 us

profile of v3, /device:TPU:0, one launch (start us, length us, event | category | flops | bytes accessed | tf_op | source)
XLA Modules:
  0.0 35.5 jit_solution(7274098262732602393)
XLA Ops:
  0.7 7.9 %exchange.1 = (f32[2,4,2048]{2,1,0:T(4,128)S(1)}, f32[6,2048]{1,0:T(8,128)S(1)}, bf16[6,2048]{1,0:T(8,128)(2,1)S(1)}, s32[1,2048]{1,0:T(1,128)S(1)}, s32[1,2048]...) custom-call(f32[2,4,2048]{2,1,0:T(4,128)} %y_ref.1, f32[6,2048]{1,0:T(8,128)} %wy_ref.1, f32[6,2048]{1,0:T(8,128)} %wx_ref.1, ...), custom_call_target="tpu_custom_call" | custom-call | flops 1000000000 | bytes 1000000 | tf_op jit(solution)/shard_map/exchange/pallas_call | solution.py:164
  8.5 0.0 copy-start
  8.5 0.0 copy-start.1
  8.5 0.0 copy-start.2
  8.5 11.5 %spread.1 = (bf16[2,1024,2048]{2,1,0:T(8,128)(2,1)S(1)}, f32[2,2,64,1024]{3,2,1,0:T(8,128)S(1)}) custom-call(f32[2,4,2048]{2,1,0:T(4,128)S(1)} %get-tuple-element.13.y_ref, f32[6,2048]{1,0:T(8,128)S(1)} %get-tuple-element.14.wy_ref, bf16[6,2048]{1,0:T(8,128)(2,1)S(1)} %get-tuple-element.15.wx_ref, s32[1,2048]{1,0:T(1,128)S(1)} %get-tuple-element.16.key_ref, ...), custom_call_target="tpu_custom_call" | custom-call | flops 12999999488 | bytes 4194304 | tf_op jit(solution)/shard_map/spread/pallas_call | solution.py:245
  20.1 0.0 copy-done
  20.1 0.0 copy-done.1
  20.1 0.0 copy-done.2
  20.1 14.7 %combine.1 = f32[2,256,128]{2,1,0:T(8,128)S(1)} custom-call(bf16[2,1024,2048]{2,1,0:T(8,128)(2,1)S(1)} %get-tuple-element.19.gg, f32[2,2,64,1024]{3,2,1,0:T(8,128)S(1)} %get-tuple-element.20.ee, bf16[2,512,1024]{2,1,0:T(8,128)(2,1)S(1)} %copy-done.2, f32[2,4,512,128]{3,2,1,0:T(8,128)S(1)} %copy-done, f32[1,512]{1,0:T(1,128)S(1)} %bitcast.3), custom_call_target="tpu_custom_call" | custom-call | flops 7000000000 | bytes 12582912 | tf_op jit(solution)/shard_map/combine/pallas_call | solution.py:407
  34.8 0.7 %copy.12 = f32[2,256,128]{2,1,0:T(8,128)} copy(f32[2,256,128]{2,1,0:T(8,128)S(1)} %combine.1) | data formatting | bytes 524288
Async XLA Ops:
  8.5 11.6 %copy-start = (f32[2,4,512,128]{3,2,1,0:T(8,128)S(1)}, f32[2,4,512,128]{3,2,1,0:T(8,128)}, u32[]{:S(2)}) copy-start(f32[2,4,512,128]{3,2,1,0:T(8,128)} %maps.1) | copy-start | bytes 6291460
  8.5 11.6 %copy-start.1 = (f32[512]{0:T(512)S(1)}, f32[512]{0:T(512)}, u32[]{:S(2)}) copy-start(f32[512]{0:T(512)} %param.16) | copy-start | bytes 6148
  8.5 11.6 %copy-start.2 = (bf16[2,512,1024]{2,1,0:T(8,128)(2,1)S(1)}, bf16[2,512,1024]{2,1,0:T(8,128)(2,1)}, u32[]{:S(2)}) copy-start(bf16[2,512,1024]{2,1,0:T(8,128)(2,1)} %constant.2.clone.tab) | copy-start | bytes 6291460

commit v4 on v3

--- a/solution.py
+++ b/solution.py
@@ -275,10 +275,6 @@
     def rows_of(a, c):
         return pl.ds(pl.multiple_of(256 * a + 128 * c, 128), 128)
 
-    for a in range(2):
-        s_all[core, a] = maps[:, :, rows_of(a, core), :]
-    row_scale = jnp.broadcast_to(dd[:, pl.ds(pl.multiple_of(y_id * 256, 256), 256)], (128, 256)).T
-    scale[...] = row_scale * dd[:, pl.ds(pl.multiple_of(row_id * 128, 128), 128)]
     pl.semaphore_wait(barrier, 3)
 
     def remote(src, dst, send, recv, dev):
@@ -295,6 +291,10 @@
     s_copies = [remote(maps.at[:, :, rows_of(a, 1 - core)], s_all.at[core, a], ssend.at[a], srecv.at[a], sib) for a in range(2)]
     for cp in s_copies:
         cp.start()
+    for a in range(2):
+        s_all[core, a] = maps[:, :, rows_of(a, core), :]
+    row_scale = jnp.broadcast_to(dd[:, pl.ds(pl.multiple_of(y_id * 256, 256), 256)], (128, 256)).T
+    scale[...] = row_scale * dd[:, pl.ds(pl.multiple_of(row_id * 128, 128), 128)]
     for hc in range(2):
         cols = pl.ds(pl.multiple_of(x_id * 256 + hc * 128, 128), 128)
         table[hc] = jnp.concatenate([tab[0, cols, :], tab[1, cols, :]], axis=0).T

time: 35.6 us -> 35.6 us (level); the launches traced: 35.5 us -> 35.9 us
  Pallas kernels: 34.1 us -> 34.5 us
    pallas_call x1, Pallas kernels: 11.5 us -> 12 us  [spread(): pl.pallas_call(spread_kernel, out_shape=(jax.ShapeDtypeStruct((2, 1024, 2...]
where the time goes in v4:
time: 35.6 us; the launch traced here: 35.9 us
  Pallas kernels  34.5 us (97%)
  local copies, waits for them, and re-layouts  0.72 us (2%)
  between operations  0.72 us (2%)
    pallas_call x1, Pallas kernels, combine(): pl.pallas_call(combine_kernel, out_shape=jax.ShapeDtypeStruct((2, 256, 12...  14.6 us
    pallas_call x1, Pallas kernels, spread(): pl.pallas_call(spread_kernel, out_shape=(jax.ShapeDtypeStruct((2, 1024, 2...  12 us
    pallas_call x1, Pallas kernels, exchange(): pl.pallas_call(exchange_kernel, out_shape=(shape(y.shape, F32), shape(wy....  7.85 us
    unnamed x7, local copies, waits for them, and re-layouts  0.72 us

profile of v4, /device:TPU:0, one launch (start us, length us, event | category | flops | bytes accessed | tf_op | source)
XLA Modules:
  0.0 35.9 jit_solution(5079216785549521355)
XLA Ops:
  0.7 7.9 %exchange.1 = (f32[2,4,2048]{2,1,0:T(4,128)S(1)}, f32[6,2048]{1,0:T(8,128)S(1)}, bf16[6,2048]{1,0:T(8,128)(2,1)S(1)}, s32[1,2048]{1,0:T(1,128)S(1)}, s32[1,2048]...) custom-call(f32[2,4,2048]{2,1,0:T(4,128)} %y_ref.1, f32[6,2048]{1,0:T(8,128)} %wy_ref.1, f32[6,2048]{1,0:T(8,128)} %wx_ref.1, ...), custom_call_target="tpu_custom_call" | custom-call | flops 1000000000 | bytes 1000000 | tf_op jit(solution)/shard_map/exchange/pallas_call | solution.py:164
  8.5 0.0 copy-start
  8.5 0.0 copy-start.1
  8.5 0.0 copy-start.2
  8.5 12.0 %spread.1 = (bf16[2,1024,2048]{2,1,0:T(8,128)(2,1)S(1)}, f32[2,2,64,1024]{3,2,1,0:T(8,128)S(1)}) custom-call(f32[2,4,2048]{2,1,0:T(4,128)S(1)} %get-tuple-element.13.y_ref, f32[6,2048]{1,0:T(8,128)S(1)} %get-tuple-element.14.wy_ref, bf16[6,2048]{1,0:T(8,128)(2,1)S(1)} %get-tuple-element.15.wx_ref, s32[1,2048]{1,0:T(1,128)S(1)} %get-tuple-element.16.key_ref, ...), custom_call_target="tpu_custom_call" | custom-call | flops 12999999488 | bytes 4194304 | tf_op jit(solution)/shard_map/spread/pallas_call | solution.py:245
  20.5 0.0 copy-done
  20.6 0.0 copy-done.1
  20.6 0.0 copy-done.2
  20.6 14.6 %combine.1 = f32[2,256,128]{2,1,0:T(8,128)S(1)} custom-call(bf16[2,1024,2048]{2,1,0:T(8,128)(2,1)S(1)} %get-tuple-element.19.gg, f32[2,2,64,1024]{3,2,1,0:T(8,128)S(1)} %get-tuple-element.20.ee, bf16[2,512,1024]{2,1,0:T(8,128)(2,1)S(1)} %copy-done.2, f32[2,4,512,128]{3,2,1,0:T(8,128)S(1)} %copy-done, f32[1,512]{1,0:T(1,128)S(1)} %bitcast.3), custom_call_target="tpu_custom_call" | custom-call | flops 7000000000 | bytes 12582912 | tf_op jit(solution)/shard_map/combine/pallas_call | solution.py:407
  35.2 0.7 %copy.12 = f32[2,256,128]{2,1,0:T(8,128)} copy(f32[2,256,128]{2,1,0:T(8,128)S(1)} %combine.1) | data formatting | bytes 524288
Async XLA Ops:
  8.5 12.0 %copy-start = (f32[2,4,512,128]{3,2,1,0:T(8,128)S(1)}, f32[2,4,512,128]{3,2,1,0:T(8,128)}, u32[]{:S(2)}) copy-start(f32[2,4,512,128]{3,2,1,0:T(8,128)} %maps.1) | copy-start | bytes 6291460
  8.5 12.0 %copy-start.1 = (f32[512]{0:T(512)S(1)}, f32[512]{0:T(512)}, u32[]{:S(2)}) copy-start(f32[512]{0:T(512)} %param.16) | copy-start | bytes 6148
  8.5 12.0 %copy-start.2 = (bf16[2,512,1024]{2,1,0:T(8,128)(2,1)S(1)}, bf16[2,512,1024]{2,1,0:T(8,128)(2,1)}, u32[]{:S(2)}) copy-start(bf16[2,512,1024]{2,1,0:T(8,128)(2,1)} %constant.2.clone.tab) | copy-start | bytes 6291460
